TPU v7x, 512 devices: a whole 4x8x8 slice. The times are simulated.
512 devices in a mesh: grid: 32 (over y, x), band: 16 (over z, core).
Axes of the slice: x: 4, y: 8, z: 8, core: 2. Of those that a mesh axis runs over, the one named last changes fastest.
Arguments:
- start: float32 [1, 4, 1, 64, 32768], P(None, None, None, 'band', 'grid'), may hold values from -6 to 6
- energies: float32 [4, 64, 32768], P(None, 'band', 'grid'), may hold values from -4 to 4
- sites: int32 [3, 1], replicated, may hold values from 0 to 31
- potential: float32 [32, 32, 32], replicated, may hold values from -4 to 400
Outputs:
- alphas: float32 [1, 1, 4], replicated
- betas: float32 [1, 1, 4], replicated
- lanczos: float32 [1, 4, 1, 64, 32768], P(None, None, None, 'band', 'grid')
All inputs are finite; a program needn't handle non-finite values.
Results may differ from a plain program's by a relative error of at most 0.0003.
Values sent between devices are 32-bit elements; how exact they have to be, the bound alone decides.
A program may use at most 64 MiB of HBM per device.

v0:
```python
import functools
import math
import jax
import jax.numpy as jnp
from jax import lax
from jax.sharding import Mesh
from jax.sharding import PartitionSpec as P

ITERS = 4
GRID = ("grid_0", "grid_1")
BAND = ("band_0", "band_1")
GRID_BAND = ("grid_0", "grid_1", "band_0", "band_1")
precise_mode = lax.Precision.HIGHEST


def one_axis_at_a_time(x, axes):
    return functools.reduce(lax.psum, axes, x)


def cas_table(grid_size):
    cells = jnp.arange(grid_size, dtype=jnp.int32)
    phase = cells[:, None] * cells[None, :] % grid_size
    angle = phase.astype(jnp.float32) * (2.0 * math.pi / grid_size)
    return jnp.cos(angle) + jnp.sin(angle)


def shift_axis(field_part, offset, axis_number):
    length = field_part.shape[axis_number]
    doubled = jnp.concatenate([field_part, field_part], axis=axis_number)
    first_index = (length - offset) % length
    return lax.dynamic_slice_in_dim(doubled, first_index, length, axis_number)


def expand_coef(values):
    return values[:, None, :, None, None]


def body(start, energies, sites, potential):
    grid_size = potential.shape[0]
    volume = grid_size * grid_size * grid_size
    atom_count, core_count, pol_count, band_local, kpoint_local = start.shape
    plane_count = grid_size // lax.axis_size(GRID)
    position = lax.axis_index(GRID)
    chain_count = core_count * pol_count * band_local
    field_count = atom_count * chain_count
    total_count = core_count * band_local * lax.axis_size(BAND) * kpoint_local * lax.axis_size(GRID)
    cas_grid = cas_table(grid_size)
    shifted = shift_axis(potential, sites[0, 0], 0)
    shifted = shift_axis(shifted, sites[1, 0], 1)
    shifted = shift_axis(shifted, sites[2, 0], 2)
    tables = [shifted]
    shifted_all = jnp.stack(tables, axis=-1)
    slab_table = lax.dynamic_slice_in_dim(shifted_all, position * plane_count, plane_count, 1)

    def moment(left, right):
        return jnp.sum(left * right, axis=(1, 3, 4)) / total_count

    start_sum = one_axis_at_a_time(moment(start, start), GRID_BAND)
    lanczos = start / expand_coef(jnp.sqrt(start_sum))
    previous = jnp.zeros_like(start)
    beta_prev = jnp.zeros((atom_count, pol_count), jnp.float32)
    alpha_list = []
    beta_list = []
    for iteration in range(ITERS):
        spread_fields = lanczos.reshape(atom_count, chain_count, plane_count, grid_size, grid_size)
        spread_over_z = jnp.einsum(
            "arpyz,wz->pywar", spread_fields, cas_grid, precision=precise_mode
        )
        spread_over_y = jnp.einsum(
            "pywar,uy->puwar", spread_over_z, cas_grid, precision=precise_mode
        )
        direct_spectrum = lax.all_to_all(
            spread_over_y.reshape(plane_count, grid_size, grid_size, field_count),
            GRID,
            split_axis=1,
            concat_axis=0,
            tiled=True,
        )
        field_shape = direct_spectrum.shape
        over_x = jnp.einsum("xvwf,tx->tvwf", direct_spectrum, cas_grid, precision=precise_mode)
        split_view = over_x.reshape(
            field_shape[0], field_shape[1], field_shape[2], atom_count, chain_count
        )
        scaled = split_view * slab_table[..., None]
        back_x = jnp.einsum("tvwar,xt->xvwar", scaled, cas_grid, precision=precise_mode)
        weighted = back_x.reshape(field_shape)
        direct_returned = lax.all_to_all(weighted, GRID, split_axis=0, concat_axis=1, tiled=True)
        fields = direct_returned.reshape(plane_count, grid_size, grid_size, atom_count, chain_count)
        over_z = jnp.einsum("pvwar,zw->pvzar", fields, cas_grid, precision=precise_mode)
        over_y = jnp.einsum("pvzar,yv->arpyz", over_z, cas_grid, precision=precise_mode)
        applied = energies[None, :, None] * lanczos - over_y.reshape(start.shape) / volume
        moments_all = (
            one_axis_at_a_time(moment(lanczos, applied), GRID_BAND),
            one_axis_at_a_time(moment(applied, applied), GRID_BAND),
            one_axis_at_a_time(moment(lanczos, lanczos), GRID_BAND),
            one_axis_at_a_time(moment(previous, previous), GRID_BAND),
            one_axis_at_a_time(moment(previous, applied), GRID_BAND),
            one_axis_at_a_time(moment(lanczos, previous), GRID_BAND),
        )
        alpha_now = moments_all[0]
        square = (
            moments_all[1]
            + alpha_now * alpha_now * moments_all[2]
            + beta_prev * beta_prev * moments_all[3]
        )
        square = square - 2.0 * alpha_now * moments_all[0] - 2.0 * beta_prev * moments_all[4]
        square = square + 2.0 * alpha_now * beta_prev * moments_all[5]
        beta_now = jnp.sqrt(square)
        remainder = applied - expand_coef(alpha_now) * lanczos - expand_coef(beta_prev) * previous
        previous = lanczos
        lanczos = remainder / expand_coef(beta_now)
        beta_prev = beta_now
        alpha_list.append(alpha_now)
        beta_list.append(beta_now)
    return (jnp.stack(alpha_list, axis=2), jnp.stack(beta_list, axis=2), lanczos)


def solution(mesh):
    split = Mesh(mesh.devices.reshape(8, 4, 8, 2), ("grid_0", "grid_1", "band_0", "band_1"))
    placed = (P(None, None, None, BAND, GRID), P(None, BAND, GRID), P(), P())
    return jax.shard_map(
        body,
        mesh=split,
        in_specs=placed,
        out_specs=(P(), P(), P(None, None, None, BAND, GRID)),
        check_vma=False,
    )
```

profile of v0, /device:TPU:1, one launch (start us, length us, event | category | flops | bytes accessed | tf_op | source)
XLA Modules:
  0.0 446.5 jit_solution(14919644235281792380)
XLA Ops:
  2.8 15.8 %psum.652 = f32[1,1]{1,0:T(1,128)} all-reduce(f32[1,1]{1,0:T(1,128)} %bitcast), channel_id=1, replica_groups=mesh['grid_0'=8,'grid_1'=4,'band_0'=8,'band_1'=2] {'grid_0'}, use_global_device_ids=true, to_apply=%region_1.2 | all-reduce | flops 1 | bytes 8 | tf_op jit(solution)/shard_map/psum | solution.py:17
  18.6 9.1 %psum.653 = f32[1,1]{1,0:T(1,128)} all-reduce(f32[1,1]{1,0:T(1,128)} %psum.652), channel_id=1, replica_groups=mesh['grid_0'=8,'grid_1'=4,'band_0'=8,'band_1'=2] {'grid_1'}, use_global_device_ids=true, to_apply=%region_2.3 | all-reduce | flops 1 | bytes 8 | tf_op jit(solution)/shard_map/psum | solution.py:17
  27.7 20.0 %psum.654 = f32[1,1]{1,0:T(1,128)} all-reduce(f32[1,1]{1,0:T(1,128)} %psum.653), channel_id=1, replica_groups=mesh['grid_0'=8,'grid_1'=4,'band_0'=8,'band_1'=2] {'band_0'}, use_global_device_ids=true, to_apply=%region_3.4 | all-reduce | flops 1 | bytes 8 | tf_op jit(solution)/shard_map/psum | solution.py:17
  47.8 12.9 %psum.655 = f32[1,1]{1,0:T(1,128)} all-reduce(f32[1,1]{1,0:T(1,128)} %psum.654), channel_id=1, replica_groups=mesh['grid_0'=8,'grid_1'=4,'band_0'=8,'band_1'=2] {'band_1'}, use_global_device_ids=true, to_apply=%region_4.5 | all-reduce | flops 1 | bytes 8 | tf_op jit(solution)/shard_map/psum | solution.py:17
  65.2 4.8 %all-to-all-start = ((f32[32,1,512]{2,1,0:T(1,128)}), f32[32,1,512]{2,1,0:T(1,128)S(1)}, u32[]{:S(2)}, u32[]{:S(2)}) async-start(f32[32,1,512]{2,1,0:T(1,128)} %reshape.373), calls=%async_computation | async-start | bytes 131072 | tf_op jit(solution)/shard_map/all_to_all | solution.py:72
  73.2 5.6 %all-to-all-done = f32[32,1,512]{2,1,0:T(1,128)S(1)} async-done(((f32[32,1,512]{2,1,0:T(1,128)}), f32[32,1,512]{2,1,0:T(1,128)S(1)}, u32[]{:S(2)}, u32[]{:S(2)}) %all-to-all-start) | async-done | bytes 65568 | tf_op jit(solution)/shard_map/all_to_all | solution.py:72
  81.6 12.2 %all_to_all.32 = f32[32,1,512]{2,1,0:T(1,128)S(1)} all-to-all(f32[32,1,512]{2,1,0:T(1,128)S(1)} %reshape.375), channel_id=1, replica_groups=mesh['grid_0'=8,'grid_1'=4,'band_0'=8,'band_1'=2] {'grid_0','grid_1'}, dimensions={0} | all-to-all | bytes 131072 | tf_op jit(solution)/shard_map/all_to_all | solution.py:87
  102.0 15.3 %all-reduce.7 = (f32[1,1]{1,0:T(1,128)}, f32[1,1]{1,0:T(1,128)}, f32[1,1]{1,0:T(1,128)}, f32[1,1]{1,0:T(1,128)}, f32[1,1]{1,0:T(1,128)}, /*index=5*/f32[1,1]{1,0:T(1,128)}) all-reduce(f32[1,1]{1,0:T(1,128)} %bitcast.24, f32[1,1]{1,0:T(1,128)} %bitcast.21, ...), channel_id=1, replica_groups=mesh['grid_0'=8,'grid_1'=4,'band_0'=8,'band_1'=2] {'grid_0'}, use_global_device_ids=true, to_apply=%region_11.12 | all-reduce | flops 6 | bytes 48 | tf_op jit(solution)/shard_map/psum | solution.py:17
  117.3 7.8 %all-reduce.11 = (f32[1,1]{1,0:T(1,128)}, f32[1,1]{1,0:T(1,128)}, f32[1,1]{1,0:T(1,128)}, f32[1,1]{1,0:T(1,128)}, f32[1,1]{1,0:T(1,128)}, /*index=5*/f32[1,1]{1,0:T(1,128)}) all-reduce(f32[1,1]{1,0:T(1,128)} %get-tuple-element.59, ...), channel_id=1, replica_groups=mesh['grid_0'=8,'grid_1'=4,'band_0'=8,'band_1'=2] {'grid_1'}, use_global_device_ids=true, to_apply=%region_12.13 | all-reduce | flops 6 | bytes 48 | tf_op jit(solution)/shard_map/psum | solution.py:17
  125.0 11.4 %all-reduce.3 = (f32[1,1]{1,0:T(1,128)}, f32[1,1]{1,0:T(1,128)}, f32[1,1]{1,0:T(1,128)}, f32[1,1]{1,0:T(1,128)}, f32[1,1]{1,0:T(1,128)}, /*index=5*/f32[1,1]{1,0:T(1,128)}) all-reduce(f32[1,1]{1,0:T(1,128)} %get-tuple-element.80, ...), channel_id=1, replica_groups=mesh['grid_0'=8,'grid_1'=4,'band_0'=8,'band_1'=2] {'band_0'}, use_global_device_ids=true, to_apply=%region_13.14 | all-reduce | flops 6 | bytes 48 | tf_op jit(solution)/shard_map/psum | solution.py:17
  136.4 14.4 %all-reduce.15 = (f32[1,1]{1,0:T(1,128)}, f32[1,1]{1,0:T(1,128)}, f32[1,1]{1,0:T(1,128)}, f32[1,1]{1,0:T(1,128)}, f32[1,1]{1,0:T(1,128)}, /*index=5*/f32[1,1]{1,0:T(1,128)}) all-reduce(f32[1,1]{1,0:T(1,128)} %get-tuple-element.38, ...), channel_id=1, replica_groups=mesh['grid_0'=8,'grid_1'=4,'band_0'=8,'band_1'=2] {'band_1'}, use_global_device_ids=true, to_apply=%region_14.15 | all-reduce | flops 6 | bytes 48 | tf_op jit(solution)/shard_map/psum | solution.py:17
  161.2 13.1 %all_to_all.33 = f32[32,1,512]{2,1,0:T(1,128)S(1)} all-to-all(f32[32,1,512]{2,1,0:T(1,128)S(1)} %reshape.377), channel_id=1, replica_groups=mesh['grid_0'=8,'grid_1'=4,'band_0'=8,'band_1'=2] {'grid_0','grid_1'}, dimensions={0} | all-to-all | bytes 131072 | tf_op jit(solution)/shard_map/all_to_all | solution.py:72
  177.1 4.0 all-to-all-start.3
  181.8 8.2 %all-to-all-done.3 = f32[32,1,512]{2,1,0:T(1,128)S(1)} async-done(((f32[32,1,512]{2,1,0:T(1,128)}), f32[32,1,512]{2,1,0:T(1,128)S(1)}, u32[]{:S(2)}, u32[]{:S(2)}) %all-to-all-start.3) | async-done | bytes 65568 | tf_op jit(solution)/shard_map/all_to_all | solution.py:87
  197.5 14.6 %all-reduce.6 = (f32[1,1]{1,0:T(1,128)}, f32[1,1]{1,0:T(1,128)}, f32[1,1]{1,0:T(1,128)}, f32[1,1]{1,0:T(1,128)}, f32[1,1]{1,0:T(1,128)}) all-reduce(f32[1,1]{1,0:T(1,128)} %bitcast.45, f32[1,1]{1,0:T(1,128)} %bitcast.42, f32[1,1]{1,0:T(1,128)} %bitcast.46, ...), channel_id=1, replica_groups=mesh['grid_0'=8,'grid_1'=4,'band_0'=8,'band_1'=2] {'grid_0'}, use_global_device_ids=true, to_apply=%region_40.41 | all-reduce | flops 5 | bytes 40 | tf_op jit(solution)/shard_map/psum | solution.py:17
  212.2 7.5 %all-reduce.10 = (f32[1,1]{1,0:T(1,128)}, f32[1,1]{1,0:T(1,128)}, f32[1,1]{1,0:T(1,128)}, f32[1,1]{1,0:T(1,128)}, f32[1,1]{1,0:T(1,128)}) all-reduce(f32[1,1]{1,0:T(1,128)} %get-tuple-element.54, f32[1,1]{1,0:T(1,128)} %get-tuple-element.55, ...), channel_id=1, replica_groups=mesh['grid_0'=8,'grid_1'=4,'band_0'=8,'band_1'=2] {'grid_1'}, use_global_device_ids=true, to_apply=%region_41.42 | all-reduce | flops 5 | bytes 40 | tf_op jit(solution)/shard_map/psum | solution.py:17
  219.7 13.1 %all-reduce.2 = (f32[1,1]{1,0:T(1,128)}, f32[1,1]{1,0:T(1,128)}, f32[1,1]{1,0:T(1,128)}, f32[1,1]{1,0:T(1,128)}, f32[1,1]{1,0:T(1,128)}) all-reduce(f32[1,1]{1,0:T(1,128)} %get-tuple-element.75, f32[1,1]{1,0:T(1,128)} %get-tuple-element.76, ...), channel_id=1, replica_groups=mesh['grid_0'=8,'grid_1'=4,'band_0'=8,'band_1'=2] {'band_0'}, use_global_device_ids=true, to_apply=%region_42.43 | all-reduce | flops 5 | bytes 40 | tf_op jit(solution)/shard_map/psum | solution.py:17
  232.8 15.3 %all-reduce.14 = (f32[1,1]{1,0:T(1,128)}, f32[1,1]{1,0:T(1,128)}, f32[1,1]{1,0:T(1,128)}, f32[1,1]{1,0:T(1,128)}, f32[1,1]{1,0:T(1,128)}) all-reduce(f32[1,1]{1,0:T(1,128)} %get-tuple-element.33, f32[1,1]{1,0:T(1,128)} %get-tuple-element.34, ...), channel_id=1, replica_groups=mesh['grid_0'=8,'grid_1'=4,'band_0'=8,'band_1'=2] {'band_1'}, use_global_device_ids=true, to_apply=%region_43.44 | all-reduce | flops 5 | bytes 40 | tf_op jit(solution)/shard_map/psum | solution.py:17
  256.9 13.0 %all_to_all.34 = f32[32,1,512]{2,1,0:T(1,128)S(1)} all-to-all(f32[32,1,512]{2,1,0:T(1,128)S(1)} %reshape.381), channel_id=1, replica_groups=mesh['grid_0'=8,'grid_1'=4,'band_0'=8,'band_1'=2] {'grid_0','grid_1'}, dimensions={0} | all-to-all | bytes 131072 | tf_op jit(solution)/shard_map/all_to_all | solution.py:72
  272.8 3.9 all-to-all-start.5
  277.3 8.3 %all-to-all-done.5 = f32[32,1,512]{2,1,0:T(1,128)S(1)} async-done(((f32[32,1,512]{2,1,0:T(1,128)}), f32[32,1,512]{2,1,0:T(1,128)S(1)}, u32[]{:S(2)}, u32[]{:S(2)}) %all-to-all-start.5) | async-done | bytes 65568 | tf_op jit(solution)/shard_map/all_to_all | solution.py:87
  293.3 14.6 %all-reduce.5 = (f32[1,1]{1,0:T(1,128)}, f32[1,1]{1,0:T(1,128)}, f32[1,1]{1,0:T(1,128)}, f32[1,1]{1,0:T(1,128)}, f32[1,1]{1,0:T(1,128)}) all-reduce(f32[1,1]{1,0:T(1,128)} %bitcast.66, f32[1,1]{1,0:T(1,128)} %bitcast.63, f32[1,1]{1,0:T(1,128)} %bitcast.67, ...), channel_id=1, replica_groups=mesh['grid_0'=8,'grid_1'=4,'band_0'=8,'band_1'=2] {'grid_0'}, use_global_device_ids=true, to_apply=%region_65.66 | all-reduce | flops 5 | bytes 40 | tf_op jit(solution)/shard_map/psum | solution.py:17
  307.9 7.5 %all-reduce.9 = (f32[1,1]{1,0:T(1,128)}, f32[1,1]{1,0:T(1,128)}, f32[1,1]{1,0:T(1,128)}, f32[1,1]{1,0:T(1,128)}, f32[1,1]{1,0:T(1,128)}) all-reduce(f32[1,1]{1,0:T(1,128)} %get-tuple-element.49, f32[1,1]{1,0:T(1,128)} %get-tuple-element.50, ...), channel_id=1, replica_groups=mesh['grid_0'=8,'grid_1'=4,'band_0'=8,'band_1'=2] {'grid_1'}, use_global_device_ids=true, to_apply=%region_66.67 | all-reduce | flops 5 | bytes 40 | tf_op jit(solution)/shard_map/psum | solution.py:17
  315.4 11.4 %all-reduce.1 = (f32[1,1]{1,0:T(1,128)}, f32[1,1]{1,0:T(1,128)}, f32[1,1]{1,0:T(1,128)}, f32[1,1]{1,0:T(1,128)}, f32[1,1]{1,0:T(1,128)}) all-reduce(f32[1,1]{1,0:T(1,128)} %get-tuple-element.70, f32[1,1]{1,0:T(1,128)} %get-tuple-element.71, ...), channel_id=1, replica_groups=mesh['grid_0'=8,'grid_1'=4,'band_0'=8,'band_1'=2] {'band_0'}, use_global_device_ids=true, to_apply=%region_67.68 | all-reduce | flops 5 | bytes 40 | tf_op jit(solution)/shard_map/psum | solution.py:17
  326.8 15.0 %all-reduce.13 = (f32[1,1]{1,0:T(1,128)}, f32[1,1]{1,0:T(1,128)}, f32[1,1]{1,0:T(1,128)}, f32[1,1]{1,0:T(1,128)}, f32[1,1]{1,0:T(1,128)}) all-reduce(f32[1,1]{1,0:T(1,128)} %get-tuple-element.28, f32[1,1]{1,0:T(1,128)} %get-tuple-element.29, ...), channel_id=1, replica_groups=mesh['grid_0'=8,'grid_1'=4,'band_0'=8,'band_1'=2] {'band_1'}, use_global_device_ids=true, to_apply=%region_68.69 | all-reduce | flops 5 | bytes 40 | tf_op jit(solution)/shard_map/psum | solution.py:17
  350.5 13.0 %all_to_all.35 = f32[32,1,512]{2,1,0:T(1,128)S(1)} all-to-all(f32[32,1,512]{2,1,0:T(1,128)S(1)} %reshape.385), channel_id=1, replica_groups=mesh['grid_0'=8,'grid_1'=4,'band_0'=8,'band_1'=2] {'grid_0','grid_1'}, dimensions={0} | all-to-all | bytes 131072 | tf_op jit(solution)/shard_map/all_to_all | solution.py:72
  366.3 3.9 all-to-all-start.7
  370.8 8.4 %all-to-all-done.7 = f32[32,1,512]{2,1,0:T(1,128)S(1)} async-done(((f32[32,1,512]{2,1,0:T(1,128)}), f32[32,1,512]{2,1,0:T(1,128)S(1)}, u32[]{:S(2)}, u32[]{:S(2)}) %all-to-all-start.7) | async-done | bytes 65568 | tf_op jit(solution)/shard_map/all_to_all | solution.py:87
  386.9 14.6 %all-reduce.4 = (f32[1,1]{1,0:T(1,128)}, f32[1,1]{1,0:T(1,128)}, f32[1,1]{1,0:T(1,128)}, f32[1,1]{1,0:T(1,128)}, f32[1,1]{1,0:T(1,128)}) all-reduce(f32[1,1]{1,0:T(1,128)} %bitcast.84, f32[1,1]{1,0:T(1,128)} %bitcast.89, f32[1,1]{1,0:T(1,128)} %bitcast.90, ...), channel_id=1, replica_groups=mesh['grid_0'=8,'grid_1'=4,'band_0'=8,'band_1'=2] {'grid_0'}, use_global_device_ids=true, to_apply=%region_85.86 | all-reduce | flops 5 | bytes 40 | tf_op jit(solution)/shard_map/psum | solution.py:17
  401.5 7.5 %all-reduce.8 = (f32[1,1]{1,0:T(1,128)}, f32[1,1]{1,0:T(1,128)}, f32[1,1]{1,0:T(1,128)}, f32[1,1]{1,0:T(1,128)}, f32[1,1]{1,0:T(1,128)}) all-reduce(f32[1,1]{1,0:T(1,128)} %get-tuple-element.44, f32[1,1]{1,0:T(1,128)} %get-tuple-element.45, ...), channel_id=1, replica_groups=mesh['grid_0'=8,'grid_1'=4,'band_0'=8,'band_1'=2] {'grid_1'}, use_global_device_ids=true, to_apply=%region_86.87 | all-reduce | flops 5 | bytes 40 | tf_op jit(solution)/shard_map/psum | solution.py:17
  409.0 13.1 %all-reduce = (f32[1,1]{1,0:T(1,128)}, f32[1,1]{1,0:T(1,128)}, f32[1,1]{1,0:T(1,128)}, f32[1,1]{1,0:T(1,128)}, f32[1,1]{1,0:T(1,128)}) all-reduce(f32[1,1]{1,0:T(1,128)} %get-tuple-element.65, f32[1,1]{1,0:T(1,128)} %get-tuple-element.66, ...), channel_id=1, replica_groups=mesh['grid_0'=8,'grid_1'=4,'band_0'=8,'band_1'=2] {'band_0'}, use_global_device_ids=true, to_apply=%region_87.88 | all-reduce | flops 5 | bytes 40 | tf_op jit(solution)/shard_map/psum | solution.py:17
  422.1 15.2 %all-reduce.12 = (f32[1,1]{1,0:T(1,128)}, f32[1,1]{1,0:T(1,128)}, f32[1,1]{1,0:T(1,128)}, f32[1,1]{1,0:T(1,128)}, f32[1,1]{1,0:T(1,128)}) all-reduce(f32[1,1]{1,0:T(1,128)} %get-tuple-element.23, f32[1,1]{1,0:T(1,128)} %get-tuple-element.24, ...), channel_id=1, replica_groups=mesh['grid_0'=8,'grid_1'=4,'band_0'=8,'band_1'=2] {'band_1'}, use_global_device_ids=true, to_apply=%region_88.89 | all-reduce | flops 5 | bytes 40 | tf_op jit(solution)/shard_map/psum | solution.py:17
  (92 shorter events, 51.6 us)
Async XLA Ops:
  0.6 60.8 %copy-start = (f32[1,4,1,4,1024]{4,3,2,1,0:T(4,128)S(1)}, f32[1,4,1,4,1024]{4,3,2,1,0:T(4,128)}, u32[]{:S(2)}) copy-start(f32[1,4,1,4,1024]{4,3,2,1,0:T(4,128)} %param.4) | copy-start | bytes 196612
  64.2 7.8 %copy-start.2 = (f32[32,32,32]{2,1,0:T(8,128)S(1)}, f32[32,32,32]{2,1,0:T(8,128)}, u32[]{:S(2)}) copy-start(f32[32,32,32]{2,1,0:T(8,128)} %param.7) | copy-start | bytes 393220
  65.1 4.9 %copy-start.3 = (s32[3,1]{0,1:T(1,128)S(1)}, s32[3,1]{0,1:T(1,128)}, u32[]{:S(2)}) copy-start(s32[3,1]{0,1:T(1,128)} %param.6) | copy-start | bytes 40
  65.2 13.7 %all-to-all-start = ((f32[32,1,512]{2,1,0:T(1,128)}), f32[32,1,512]{2,1,0:T(1,128)S(1)}, u32[]{:S(2)}, u32[]{:S(2)}) async-start(f32[32,1,512]{2,1,0:T(1,128)} %reshape.373), calls=%async_computation | async-start | bytes 131072 | tf_op jit(solution)/shard_map/all_to_all | solution.py:72
  97.3 0.8 copy-start.1
  177.1 12.8 %all-to-all-start.3 = ((f32[32,1,512]{2,1,0:T(1,128)}), f32[32,1,512]{2,1,0:T(1,128)S(1)}, u32[]{:S(2)}, u32[]{:S(2)}) async-start(f32[32,1,512]{2,1,0:T(1,128)} %reshape.379), calls=%async_computation.3 | async-start | bytes 131072 | tf_op jit(solution)/shard_map/all_to_all | solution.py:87
  272.8 12.8 %all-to-all-start.5 = ((f32[32,1,512]{2,1,0:T(1,128)}), f32[32,1,512]{2,1,0:T(1,128)S(1)}, u32[]{:S(2)}, u32[]{:S(2)}) async-start(f32[32,1,512]{2,1,0:T(1,128)} %reshape.383), calls=%async_computation.5 | async-start | bytes 131072 | tf_op jit(solution)/shard_map/all_to_all | solution.py:87
  366.3 12.8 %all-to-all-start.7 = ((f32[32,1,512]{2,1,0:T(1,128)}), f32[32,1,512]{2,1,0:T(1,128)S(1)}, u32[]{:S(2)}, u32[]{:S(2)}) async-start(f32[32,1,512]{2,1,0:T(1,128)} %reshape.387), calls=%async_computation.7 | async-start | bytes 131072 | tf_op jit(solution)/shard_map/all_to_all | solution.py:87
where the time goes:
time: 448 us; the launch traced here: 447 us
  blocking collectives  307 us (69%)
  between operations  40.5 us (9%)
  waiting for transfers between devices  30.5 us (7%)
  matrix products  24.7 us (6%)
  other arithmetic  17.8 us (4%)
  starting transfers between devices  16.6 us (4%)
  local copies, waits for them, and re-layouts  9.11 us (2%)
    psum x20, blocking collectives, one_axis_at_a_time(): return functools.reduce(lax.psum, axes, x)  256 us
    all_to_all x3, blocking collectives, body(): lax.all_to_all(spread_over_y.reshape(plane_count, grid_size, grid_size, f...  39 us
    all_to_all x3, waiting for transfers between devices, body(): lax.all_to_all(weighted, GRID, split_axis=0, concat_axis=1, tiled=True)  24.8 us
    all_to_all x1, blocking collectives, body(): lax.all_to_all(weighted, GRID, split_axis=0, concat_axis=1, tiled=True)  12.2 us
    all_to_all x3, starting transfers between devices, body(): lax.all_to_all(weighted, GRID, split_axis=0, concat_axis=1, tiled=True)  11.7 us
  transfers between devices with their start and end apart: 4, of which 4 were waited for; matrix products, arithmetic and copies ran while one was open for 0% of the time, Pallas kernels for 0%

commit v1 on v0

--- a/solution.py
+++ b/solution.py
@@ -84,7 +84,9 @@
         scaled = split_view * slab_table[..., None]
         back_x = jnp.einsum("tvwar,xt->xvwar", scaled, cas_grid, precision=precise_mode)
         weighted = back_x.reshape(field_shape)
-        direct_returned = lax.all_to_all(weighted, GRID, split_axis=0, concat_axis=1, tiled=True)
+        cells_2 = jnp.split(weighted, lax.axis_size(GRID), axis=0)
+        incoming = lax.all_to_all(jnp.stack(cells_2), GRID, 0, 0)
+        direct_returned = jnp.concatenate(incoming, axis=1)
         fields = direct_returned.reshape(plane_count, grid_size, grid_size, atom_count, chain_count)
         over_z = jnp.einsum("pvwar,zw->pvzar", fields, cas_grid, precision=precise_mode)
         over_y = jnp.einsum("pvzar,yv->arpyz", over_z, cas_grid, precision=precise_mode)

time: 448 us -> 450 us (level)
  no operation moved by 1% of the time
where the time goes in v1:
time: 450 us; the launch traced here: 448 us
  blocking collectives  308 us (68%)
  between operations  41.6 us (9%)
  waiting for transfers between devices  30.5 us (7%)
  matrix products  24.7 us (5%)
  other arithmetic  17.8 us (4%)
  starting transfers between devices  16.6 us (4%)
  local copies, waits for them, and re-layouts  9.71 us (2%)
    psum x20, blocking collectives, one_axis_at_a_time(): return functools.reduce(lax.psum, axes, x)  256 us
    all_to_all x3, blocking collectives, body(): lax.all_to_all(spread_over_y.reshape(plane_count, grid_size, grid_size, f...  39.1 us
    all_to_all x3, waiting for transfers between devices, body(): incoming = lax.all_to_all(jnp.stack(cells_2), GRID, 0, 0)  24.8 us
    all_to_all x1, blocking collectives, body(): incoming = lax.all_to_all(jnp.stack(cells_2), GRID, 0, 0)  12.2 us
    all_to_all x3, starting transfers between devices, body(): incoming = lax.all_to_all(jnp.stack(cells_2), GRID, 0, 0)  11.7 us
  transfers between devices with their start and end apart: 4, of which 4 were waited for; matrix products, arithmetic and copies ran while one was open for 0% of the time, Pallas kernels for 0%

profile of v1, /device:TPU:1, one launch (start us, length us, event | category | flops | bytes accessed | tf_op | source)
XLA Modules:
  0.0 448.4 jit_solution(15229270374166463934)
XLA Ops:
  2.8 15.8 %psum.652 = f32[1,1]{1,0:T(1,128)} all-reduce(f32[1,1]{1,0:T(1,128)} %bitcast), channel_id=1, replica_groups=mesh['grid_0'=8,'grid_1'=4,'band_0'=8,'band_1'=2] {'grid_0'}, use_global_device_ids=true, to_apply=%region_1.2 | all-reduce | flops 1 | bytes 8 | tf_op jit(solution)/shard_map/psum | solution.py:17
  18.6 9.1 %psum.653 = f32[1,1]{1,0:T(1,128)} all-reduce(f32[1,1]{1,0:T(1,128)} %psum.652), channel_id=1, replica_groups=mesh['grid_0'=8,'grid_1'=4,'band_0'=8,'band_1'=2] {'grid_1'}, use_global_device_ids=true, to_apply=%region_2.3 | all-reduce | flops 1 | bytes 8 | tf_op jit(solution)/shard_map/psum | solution.py:17
  27.7 20.0 %psum.654 = f32[1,1]{1,0:T(1,128)} all-reduce(f32[1,1]{1,0:T(1,128)} %psum.653), channel_id=1, replica_groups=mesh['grid_0'=8,'grid_1'=4,'band_0'=8,'band_1'=2] {'band_0'}, use_global_device_ids=true, to_apply=%region_3.4 | all-reduce | flops 1 | bytes 8 | tf_op jit(solution)/shard_map/psum | solution.py:17
  47.8 12.9 %psum.655 = f32[1,1]{1,0:T(1,128)} all-reduce(f32[1,1]{1,0:T(1,128)} %psum.654), channel_id=1, replica_groups=mesh['grid_0'=8,'grid_1'=4,'band_0'=8,'band_1'=2] {'band_1'}, use_global_device_ids=true, to_apply=%region_4.5 | all-reduce | flops 1 | bytes 8 | tf_op jit(solution)/shard_map/psum | solution.py:17
  65.2 4.8 %all-to-all-start = ((f32[32,1,512]{2,1,0:T(1,128)}), f32[32,1,512]{2,1,0:T(1,128)S(1)}, u32[]{:S(2)}, u32[]{:S(2)}) async-start(f32[32,1,512]{2,1,0:T(1,128)} %reshape.597), calls=%async_computation | async-start | bytes 131072 | tf_op jit(solution)/shard_map/all_to_all | solution.py:72
  73.2 5.6 %all-to-all-done = f32[32,1,512]{2,1,0:T(1,128)S(1)} async-done(((f32[32,1,512]{2,1,0:T(1,128)}), f32[32,1,512]{2,1,0:T(1,128)S(1)}, u32[]{:S(2)}, u32[]{:S(2)}) %all-to-all-start) | async-done | bytes 65568 | tf_op jit(solution)/shard_map/all_to_all | solution.py:72
  82.0 12.2 %all_to_all.56 = f32[32,1,512]{2,1,0:T(1,128)S(1)} all-to-all(f32[32,1,512]{2,1,0:T(1,128)S(1)} %reshape.599), channel_id=1, replica_groups=mesh['grid_0'=8,'grid_1'=4,'band_0'=8,'band_1'=2] {'grid_0','grid_1'}, dimensions={0} | all-to-all | bytes 131072 | tf_op jit(solution)/shard_map/all_to_all | solution.py:88
  102.4 15.4 %all-reduce.7 = (f32[1,1]{1,0:T(1,128)}, f32[1,1]{1,0:T(1,128)}, f32[1,1]{1,0:T(1,128)}, f32[1,1]{1,0:T(1,128)}, f32[1,1]{1,0:T(1,128)}, /*index=5*/f32[1,1]{1,0:T(1,128)}) all-reduce(f32[1,1]{1,0:T(1,128)} %bitcast.55, f32[1,1]{1,0:T(1,128)} %bitcast.52, ...), channel_id=1, replica_groups=mesh['grid_0'=8,'grid_1'=4,'band_0'=8,'band_1'=2] {'grid_0'}, use_global_device_ids=true, to_apply=%region_11.12 | all-reduce | flops 6 | bytes 48 | tf_op jit(solution)/shard_map/psum | solution.py:17
  117.8 7.8 %all-reduce.11 = (f32[1,1]{1,0:T(1,128)}, f32[1,1]{1,0:T(1,128)}, f32[1,1]{1,0:T(1,128)}, f32[1,1]{1,0:T(1,128)}, f32[1,1]{1,0:T(1,128)}, /*index=5*/f32[1,1]{1,0:T(1,128)}) all-reduce(f32[1,1]{1,0:T(1,128)} %get-tuple-element.59, ...), channel_id=1, replica_groups=mesh['grid_0'=8,'grid_1'=4,'band_0'=8,'band_1'=2] {'grid_1'}, use_global_device_ids=true, to_apply=%region_12.13 | all-reduce | flops 6 | bytes 48 | tf_op jit(solution)/shard_map/psum | solution.py:17
  125.6 11.4 %all-reduce.3 = (f32[1,1]{1,0:T(1,128)}, f32[1,1]{1,0:T(1,128)}, f32[1,1]{1,0:T(1,128)}, f32[1,1]{1,0:T(1,128)}, f32[1,1]{1,0:T(1,128)}, /*index=5*/f32[1,1]{1,0:T(1,128)}) all-reduce(f32[1,1]{1,0:T(1,128)} %get-tuple-element.80, ...), channel_id=1, replica_groups=mesh['grid_0'=8,'grid_1'=4,'band_0'=8,'band_1'=2] {'band_0'}, use_global_device_ids=true, to_apply=%region_13.14 | all-reduce | flops 6 | bytes 48 | tf_op jit(solution)/shard_map/psum | solution.py:17
  137.0 14.4 %all-reduce.15 = (f32[1,1]{1,0:T(1,128)}, f32[1,1]{1,0:T(1,128)}, f32[1,1]{1,0:T(1,128)}, f32[1,1]{1,0:T(1,128)}, f32[1,1]{1,0:T(1,128)}, /*index=5*/f32[1,1]{1,0:T(1,128)}) all-reduce(f32[1,1]{1,0:T(1,128)} %get-tuple-element.38, ...), channel_id=1, replica_groups=mesh['grid_0'=8,'grid_1'=4,'band_0'=8,'band_1'=2] {'band_1'}, use_global_device_ids=true, to_apply=%region_14.15 | all-reduce | flops 6 | bytes 48 | tf_op jit(solution)/shard_map/psum | solution.py:17
  161.8 13.1 %all_to_all.57 = f32[32,1,512]{2,1,0:T(1,128)S(1)} all-to-all(f32[32,1,512]{2,1,0:T(1,128)S(1)} %reshape.601), channel_id=1, replica_groups=mesh['grid_0'=8,'grid_1'=4,'band_0'=8,'band_1'=2] {'grid_0','grid_1'}, dimensions={0} | all-to-all | bytes 131072 | tf_op jit(solution)/shard_map/all_to_all | solution.py:72
  178.1 4.0 all-to-all-start.3
  182.8 8.2 %all-to-all-done.3 = f32[32,1,512]{2,1,0:T(1,128)S(1)} async-done(((f32[32,1,512]{2,1,0:T(1,128)}), f32[32,1,512]{2,1,0:T(1,128)S(1)}, u32[]{:S(2)}, u32[]{:S(2)}) %all-to-all-start.3) | async-done | bytes 65568 | tf_op jit(solution)/shard_map/all_to_all | solution.py:88
  198.5 14.7 %all-reduce.6 = (f32[1,1]{1,0:T(1,128)}, f32[1,1]{1,0:T(1,128)}, f32[1,1]{1,0:T(1,128)}, f32[1,1]{1,0:T(1,128)}, f32[1,1]{1,0:T(1,128)}) all-reduce(f32[1,1]{1,0:T(1,128)} %bitcast.107, f32[1,1]{1,0:T(1,128)} %bitcast.104, f32[1,1]{1,0:T(1,128)} %bitcast.108, ...), channel_id=1, replica_groups=mesh['grid_0'=8,'grid_1'=4,'band_0'=8,'band_1'=2] {'grid_0'}, use_global_device_ids=true, to_apply=%region_40.41 | all-reduce | flops 5 | bytes 40 | tf_op jit(solution)/shard_map/psum | solution.py:17
  213.2 7.5 %all-reduce.10 = (f32[1,1]{1,0:T(1,128)}, f32[1,1]{1,0:T(1,128)}, f32[1,1]{1,0:T(1,128)}, f32[1,1]{1,0:T(1,128)}, f32[1,1]{1,0:T(1,128)}) all-reduce(f32[1,1]{1,0:T(1,128)} %get-tuple-element.54, f32[1,1]{1,0:T(1,128)} %get-tuple-element.55, ...), channel_id=1, replica_groups=mesh['grid_0'=8,'grid_1'=4,'band_0'=8,'band_1'=2] {'grid_1'}, use_global_device_ids=true, to_apply=%region_41.42 | all-reduce | flops 5 | bytes 40 | tf_op jit(solution)/shard_map/psum | solution.py:17
  220.7 13.1 %all-reduce.2 = (f32[1,1]{1,0:T(1,128)}, f32[1,1]{1,0:T(1,128)}, f32[1,1]{1,0:T(1,128)}, f32[1,1]{1,0:T(1,128)}, f32[1,1]{1,0:T(1,128)}) all-reduce(f32[1,1]{1,0:T(1,128)} %get-tuple-element.75, f32[1,1]{1,0:T(1,128)} %get-tuple-element.76, ...), channel_id=1, replica_groups=mesh['grid_0'=8,'grid_1'=4,'band_0'=8,'band_1'=2] {'band_0'}, use_global_device_ids=true, to_apply=%region_42.43 | all-reduce | flops 5 | bytes 40 | tf_op jit(solution)/shard_map/psum | solution.py:17
  233.7 15.3 %all-reduce.14 = (f32[1,1]{1,0:T(1,128)}, f32[1,1]{1,0:T(1,128)}, f32[1,1]{1,0:T(1,128)}, f32[1,1]{1,0:T(1,128)}, f32[1,1]{1,0:T(1,128)}) all-reduce(f32[1,1]{1,0:T(1,128)} %get-tuple-element.33, f32[1,1]{1,0:T(1,128)} %get-tuple-element.34, ...), channel_id=1, replica_groups=mesh['grid_0'=8,'grid_1'=4,'band_0'=8,'band_1'=2] {'band_1'}, use_global_device_ids=true, to_apply=%region_43.44 | all-reduce | flops 5 | bytes 40 | tf_op jit(solution)/shard_map/psum | solution.py:17
  257.9 13.0 %all_to_all.58 = f32[32,1,512]{2,1,0:T(1,128)S(1)} all-to-all(f32[32,1,512]{2,1,0:T(1,128)S(1)} %reshape.605), channel_id=1, replica_groups=mesh['grid_0'=8,'grid_1'=4,'band_0'=8,'band_1'=2] {'grid_0','grid_1'}, dimensions={0} | all-to-all | bytes 131072 | tf_op jit(solution)/shard_map/all_to_all | solution.py:72
  274.2 3.9 all-to-all-start.5
  278.7 8.3 %all-to-all-done.5 = f32[32,1,512]{2,1,0:T(1,128)S(1)} async-done(((f32[32,1,512]{2,1,0:T(1,128)}), f32[32,1,512]{2,1,0:T(1,128)S(1)}, u32[]{:S(2)}, u32[]{:S(2)}) %all-to-all-start.5) | async-done | bytes 65568 | tf_op jit(solution)/shard_map/all_to_all | solution.py:88
  294.7 14.7 %all-reduce.5 = (f32[1,1]{1,0:T(1,128)}, f32[1,1]{1,0:T(1,128)}, f32[1,1]{1,0:T(1,128)}, f32[1,1]{1,0:T(1,128)}, f32[1,1]{1,0:T(1,128)}) all-reduce(f32[1,1]{1,0:T(1,128)} %bitcast.159, f32[1,1]{1,0:T(1,128)} %bitcast.156, f32[1,1]{1,0:T(1,128)} %bitcast.160, ...), channel_id=1, replica_groups=mesh['grid_0'=8,'grid_1'=4,'band_0'=8,'band_1'=2] {'grid_0'}, use_global_device_ids=true, to_apply=%region_65.66 | all-reduce | flops 5 | bytes 40 | tf_op jit(solution)/shard_map/psum | solution.py:17
  309.4 7.5 %all-reduce.9 = (f32[1,1]{1,0:T(1,128)}, f32[1,1]{1,0:T(1,128)}, f32[1,1]{1,0:T(1,128)}, f32[1,1]{1,0:T(1,128)}, f32[1,1]{1,0:T(1,128)}) all-reduce(f32[1,1]{1,0:T(1,128)} %get-tuple-element.49, f32[1,1]{1,0:T(1,128)} %get-tuple-element.50, ...), channel_id=1, replica_groups=mesh['grid_0'=8,'grid_1'=4,'band_0'=8,'band_1'=2] {'grid_1'}, use_global_device_ids=true, to_apply=%region_66.67 | all-reduce | flops 5 | bytes 40 | tf_op jit(solution)/shard_map/psum | solution.py:17
  316.9 11.4 %all-reduce.1 = (f32[1,1]{1,0:T(1,128)}, f32[1,1]{1,0:T(1,128)}, f32[1,1]{1,0:T(1,128)}, f32[1,1]{1,0:T(1,128)}, f32[1,1]{1,0:T(1,128)}) all-reduce(f32[1,1]{1,0:T(1,128)} %get-tuple-element.70, f32[1,1]{1,0:T(1,128)} %get-tuple-element.71, ...), channel_id=1, replica_groups=mesh['grid_0'=8,'grid_1'=4,'band_0'=8,'band_1'=2] {'band_0'}, use_global_device_ids=true, to_apply=%region_67.68 | all-reduce | flops 5 | bytes 40 | tf_op jit(solution)/shard_map/psum | solution.py:17
  328.3 15.0 %all-reduce.13 = (f32[1,1]{1,0:T(1,128)}, f32[1,1]{1,0:T(1,128)}, f32[1,1]{1,0:T(1,128)}, f32[1,1]{1,0:T(1,128)}, f32[1,1]{1,0:T(1,128)}) all-reduce(f32[1,1]{1,0:T(1,128)} %get-tuple-element.28, f32[1,1]{1,0:T(1,128)} %get-tuple-element.29, ...), channel_id=1, replica_groups=mesh['grid_0'=8,'grid_1'=4,'band_0'=8,'band_1'=2] {'band_1'}, use_global_device_ids=true, to_apply=%region_68.69 | all-reduce | flops 5 | bytes 40 | tf_op jit(solution)/shard_map/psum | solution.py:17
  352.0 13.0 %all_to_all.59 = f32[32,1,512]{2,1,0:T(1,128)S(1)} all-to-all(f32[32,1,512]{2,1,0:T(1,128)S(1)} %reshape.609), channel_id=1, replica_groups=mesh['grid_0'=8,'grid_1'=4,'band_0'=8,'band_1'=2] {'grid_0','grid_1'}, dimensions={0} | all-to-all | bytes 131072 | tf_op jit(solution)/shard_map/all_to_all | solution.py:72
  368.2 3.9 all-to-all-start.7
  372.6 8.4 %all-to-all-done.7 = f32[32,1,512]{2,1,0:T(1,128)S(1)} async-done(((f32[32,1,512]{2,1,0:T(1,128)}), f32[32,1,512]{2,1,0:T(1,128)S(1)}, u32[]{:S(2)}, u32[]{:S(2)}) %all-to-all-start.7) | async-done | bytes 65568 | tf_op jit(solution)/shard_map/all_to_all | solution.py:88
  388.8 14.6 %all-reduce.4 = (f32[1,1]{1,0:T(1,128)}, f32[1,1]{1,0:T(1,128)}, f32[1,1]{1,0:T(1,128)}, f32[1,1]{1,0:T(1,128)}, f32[1,1]{1,0:T(1,128)}) all-reduce(f32[1,1]{1,0:T(1,128)} %bitcast.208, f32[1,1]{1,0:T(1,128)} %bitcast.213, f32[1,1]{1,0:T(1,128)} %bitcast.214, ...), channel_id=1, replica_groups=mesh['grid_0'=8,'grid_1'=4,'band_0'=8,'band_1'=2] {'grid_0'}, use_global_device_ids=true, to_apply=%region_85.86 | all-reduce | flops 5 | bytes 40 | tf_op jit(solution)/shard_map/psum | solution.py:17
  403.4 7.5 %all-reduce.8 = (f32[1,1]{1,0:T(1,128)}, f32[1,1]{1,0:T(1,128)}, f32[1,1]{1,0:T(1,128)}, f32[1,1]{1,0:T(1,128)}, f32[1,1]{1,0:T(1,128)}) all-reduce(f32[1,1]{1,0:T(1,128)} %get-tuple-element.44, f32[1,1]{1,0:T(1,128)} %get-tuple-element.45, ...), channel_id=1, replica_groups=mesh['grid_0'=8,'grid_1'=4,'band_0'=8,'band_1'=2] {'grid_1'}, use_global_device_ids=true, to_apply=%region_86.87 | all-reduce | flops 5 | bytes 40 | tf_op jit(solution)/shard_map/psum | solution.py:17
  410.9 13.1 %all-reduce = (f32[1,1]{1,0:T(1,128)}, f32[1,1]{1,0:T(1,128)}, f32[1,1]{1,0:T(1,128)}, f32[1,1]{1,0:T(1,128)}, f32[1,1]{1,0:T(1,128)}) all-reduce(f32[1,1]{1,0:T(1,128)} %get-tuple-element.65, f32[1,1]{1,0:T(1,128)} %get-tuple-element.66, ...), channel_id=1, replica_groups=mesh['grid_0'=8,'grid_1'=4,'band_0'=8,'band_1'=2] {'band_0'}, use_global_device_ids=true, to_apply=%region_87.88 | all-reduce | flops 5 | bytes 40 | tf_op jit(solution)/shard_map/psum | solution.py:17
  424.0 15.2 %all-reduce.12 = (f32[1,1]{1,0:T(1,128)}, f32[1,1]{1,0:T(1,128)}, f32[1,1]{1,0:T(1,128)}, f32[1,1]{1,0:T(1,128)}, f32[1,1]{1,0:T(1,128)}) all-reduce(f32[1,1]{1,0:T(1,128)} %get-tuple-element.23, f32[1,1]{1,0:T(1,128)} %get-tuple-element.24, ...), channel_id=1, replica_groups=mesh['grid_0'=8,'grid_1'=4,'band_0'=8,'band_1'=2] {'band_1'}, use_global_device_ids=true, to_apply=%region_88.89 | all-reduce | flops 5 | bytes 40 | tf_op jit(solution)/shard_map/psum | solution.py:17
  (228 shorter events, 52.2 us)
Async XLA Ops:
  0.6 60.8 %copy-start = (f32[1,4,1,4,1024]{4,3,2,1,0:T(4,128)S(1)}, f32[1,4,1,4,1024]{4,3,2,1,0:T(4,128)}, u32[]{:S(2)}) copy-start(f32[1,4,1,4,1024]{4,3,2,1,0:T(4,128)} %param.4) | copy-start | bytes 196612
  64.2 7.8 %copy-start.2 = (f32[32,32,32]{2,1,0:T(8,128)S(1)}, f32[32,32,32]{2,1,0:T(8,128)}, u32[]{:S(2)}) copy-start(f32[32,32,32]{2,1,0:T(8,128)} %param.7) | copy-start | bytes 393220
  65.1 4.9 %copy-start.3 = (s32[3,1]{0,1:T(1,128)S(1)}, s32[3,1]{0,1:T(1,128)}, u32[]{:S(2)}) copy-start(s32[3,1]{0,1:T(1,128)} %param.6) | copy-start | bytes 40
  65.2 13.7 %all-to-all-start = ((f32[32,1,512]{2,1,0:T(1,128)}), f32[32,1,512]{2,1,0:T(1,128)S(1)}, u32[]{:S(2)}, u32[]{:S(2)}) async-start(f32[32,1,512]{2,1,0:T(1,128)} %reshape.597), calls=%async_computation | async-start | bytes 131072 | tf_op jit(solution)/shard_map/all_to_all | solution.py:72
  97.8 0.8 copy-start.1
  178.1 12.8 %all-to-all-start.3 = ((f32[32,1,512]{2,1,0:T(1,128)}), f32[32,1,512]{2,1,0:T(1,128)S(1)}, u32[]{:S(2)}, u32[]{:S(2)}) async-start(f32[32,1,512]{2,1,0:T(1,128)} %reshape.603), calls=%async_computation.3 | async-start | bytes 131072 | tf_op jit(solution)/shard_map/all_to_all | solution.py:88
  274.2 12.8 %all-to-all-start.5 = ((f32[32,1,512]{2,1,0:T(1,128)}), f32[32,1,512]{2,1,0:T(1,128)S(1)}, u32[]{:S(2)}, u32[]{:S(2)}) async-start(f32[32,1,512]{2,1,0:T(1,128)} %reshape.607), calls=%async_computation.5 | async-start | bytes 131072 | tf_op jit(solution)/shard_map/all_to_all | solution.py:88
  368.2 12.8 %all-to-all-start.7 = ((f32[32,1,512]{2,1,0:T(1,128)}), f32[32,1,512]{2,1,0:T(1,128)S(1)}, u32[]{:S(2)}, u32[]{:S(2)}) async-start(f32[32,1,512]{2,1,0:T(1,128)} %reshape.611), calls=%async_computation.7 | async-start | bytes 131072 | tf_op jit(solution)/shard_map/all_to_all | solution.py:88
